TPU v7x, 512 devices: a whole 4x4x16 slice. The times are simulated.
512 devices in a mesh: dp: 64 (over z_lo, x, core), ens: 8 (over y, z_hi).
Axes of the slice: x: 4, y: 4, z: 16 (z_hi: 2, z_lo: 8; z = z_hi * 8 + z_lo), core: 2. Of those that a mesh axis runs over, the one named last changes fastest.
Arguments:
- embeddings: bfloat16 [49152, 1024], P('dp'), may hold values from -6 to 6
- valid_mask: int32 [49152], P('dp'), may hold values 0 or 1
- first_weight: bfloat16 [8, 1024, 4096], P(None, 'dp', 'ens'), may hold values from -0.1875 to 0.1875
- second_weight: bfloat16 [8, 4096, 128], P(None, 'ens'), may hold values from -0.09375 to 0.09375
- thresholds: int32 [8], replicated, may hold values from -256 to 256
Outputs:
- mean_logits: float32 [49152, 128], P('dp')
- kept_share: float32 [8], P('ens')
- agree_share: float32 [8], P('ens')
All inputs are finite; a program needn't handle non-finite values. No bound on the sum of `valid_mask` on one device may be relied on, other than what follows from the above.
Results may differ from a plain program's by a relative error of at most 0.0044.
Values may be sent and summed in bfloat16 or wider, within the bound.
A program may use at most 64 MiB of HBM per device.

v0:
```python
import jax
import jax.numpy as jnp
from jax import lax
from jax.sharding import PartitionSpec as P


def split_up(shard, dim, size):
    shape = shard.shape
    blocks = shard.reshape(*shape[:dim], size, shape[dim] // size, *shape[dim + 1 :])
    return jnp.moveaxis(blocks, dim, 0)


def cut_rows(length, count):
    lap = length // count
    if lap >= 8:
        lap -= lap % 8
    return [lap * k for k in range(1, count)]


def in_order(blocks, dim):
    shape = list(blocks.shape[1:])
    shape[dim] *= blocks.shape[0]
    return jnp.moveaxis(blocks, 0, dim).reshape(shape)


def several_exchanges(shard, axis, pieces, split_dim, concat_dim):
    blocks = split_up(shard, split_dim, lax.axis_size(axis))
    split_at = max(range(1, max(2, blocks.ndim - 1)), key=lambda d: blocks.shape[d])
    done = []
    for section in jnp.split(blocks, cut_rows(blocks.shape[split_at], pieces), axis=split_at):
        if section.size:
            done.append(lax.all_to_all(section, axis, split_axis=0, concat_axis=0, tiled=True))
    return in_order(jnp.concatenate(done, axis=split_at), concat_dim)


def from_everyone(shard, axis):
    copies = jnp.broadcast_to(shard, (lax.axis_size(axis), *shard.shape))
    return lax.all_to_all(copies, axis, split_axis=0, concat_axis=0, tiled=True)


def over_copies(shard, axis):
    everything = from_everyone(shard, axis)
    return jnp.sum(everything.astype(jnp.float32), axis=0)


def of_everyone(shard, axis):
    return from_everyone(shard, axis).sum(axis=0)


def in_one(arrays, axis):
    ends = [0]
    for a in arrays:
        ends.append(ends[-1] + a.size)
    total = of_everyone(jnp.concatenate([a.ravel() for a in arrays]), axis)
    return tuple((total[b:e].reshape(a.shape) for a, b, e in zip(arrays, ends, ends[1:])))


def on_device(embeddings, valid_mask, first_weight, second_weight, thresholds):
    member = lax.axis_index("ens")
    own_first = lax.all_to_all(first_weight, "ens", split_axis=0, concat_axis=2, tiled=True)
    own_second = several_exchanges(second_weight, "ens", 2, 0, 1)
    full_first = lax.all_gather(own_first[0], "dp", axis=0, tiled=True)
    hidden = jnp.maximum(
        jnp.dot(embeddings, full_first, preferred_element_type=jnp.float32), 0.0
    ).astype(jnp.bfloat16)
    logits_own = jnp.dot(hidden, own_second[0], preferred_element_type=jnp.float32)
    classes = logits_own.shape[1]
    levels = jnp.arange(classes, dtype=jnp.float32)
    grades = (2.0 * levels / (classes - 1) - 1.0) * jnp.sqrt(jnp.float32(3.0 / classes))
    scores = jnp.dot(logits_own, grades, precision=lax.Precision.HIGHEST)
    cutoffs = thresholds.astype(jnp.float32) / 256.0
    own_cutoff = lax.dynamic_index_in_dim(cutoffs, member, 0, keepdims=False)
    validity = valid_mask.astype(jnp.float32)
    kept_soft = validity * jax.nn.sigmoid(4.0 * (scores - own_cutoff))
    mean_logits = (
        over_copies(logits_own.astype(jnp.bfloat16), "ens").astype(jnp.float32)
        / first_weight.shape[0]
    )
    ens_score = jnp.dot(mean_logits, grades, precision=lax.Precision.HIGHEST)
    ens_kept = jax.nn.sigmoid(4.0 * (ens_score - jnp.mean(cutoffs)))
    agree_local = jnp.sum(kept_soft * ens_kept)
    kept_total, agree_total = in_one((jnp.sum(kept_soft), agree_local), "dp")
    shard_docs = embeddings.shape[0]
    return (
        mean_logits,
        (kept_total / shard_docs).reshape(1),
        (agree_total / shard_docs).reshape(1),
    )


def solution(mesh):
    return jax.shard_map(
        on_device,
        mesh=mesh,
        in_specs=(P("dp", None), P("dp"), P(None, "dp", "ens"), P(None, "ens", None), P()),
        out_specs=(P("dp", None), P("ens"), P("ens")),
        check_vma=False,
    )
```

profile of v0, /device:TPU:1, one launch (start us, length us, event | category | flops | bytes accessed | tf_op | source)
XLA Modules:
  0.0 333.6 jit_solution(111445874965293776)
XLA Ops:
  7.2 0.0 copy-start
  7.2 0.0 all-gather.2.cloned.1.call-start
  7.2 32.7 %all_to_all.36 = bf16[8,16,512]{2,1,0:T(8,128)(2,1)S(1)} all-to-all(bf16[8,16,512]{2,1,0:T(8,128)(2,1)} %param.7), channel_id=1, replica_groups=mesh['dp'=64,'ens'=8] {'ens'}, dimensions={0} | all-to-all | bytes 262144 | tf_op jit(solution)/shard_map/all_to_all | solution.py:60
  39.9 0.7 copy.16
  40.5 0.0 all-gather.2.cloned.1.call-update
  40.6 1.3 fusion.12
  41.9 19.8 %all_to_all.37 = bf16[8,1,256,128]{3,2,1,0:T(8,128)(2,1)S(1)} all-to-all(bf16[8,1,256,128]{3,2,1,0:T(8,128)(2,1)S(1)} %get-tuple-element.6), channel_id=1, replica_groups=mesh['dp'=64,'ens'=8] {'ens'}, dimensions={0} | all-to-all | bytes 1048576 | tf_op jit(solution)/shard_map/all_to_all | solution.py:32
  61.7 27.5 %all_to_all.38 = bf16[8,1,256,128]{3,2,1,0:T(8,128)(2,1)S(1)} all-to-all(bf16[8,1,256,128]{3,2,1,0:T(8,128)(2,1)S(1)} %get-tuple-element.5), channel_id=1, replica_groups=mesh['dp'=64,'ens'=8] {'ens'}, dimensions={0} | all-to-all | bytes 1048576 | tf_op jit(solution)/shard_map/all_to_all | solution.py:32
  89.2 0.1 pad_maximum_fusion
  89.3 104.5 %all-gather.2.cloned.1.call-done = bf16[1024,4096]{1,0:T(8,128)(2,1)} async-done(((bf16[16,4096]{1,0:T(8,128)(2,1)}), bf16[1024,4096]{1,0:T(8,128)(2,1)}) %all-gather.2.cloned.1.call-update) | async-done | bytes 8388624 | tf_op jit(solution)/shard_map/all_gather | solution.py:62
  193.7 0.0 copy-done
  193.8 11.8 %fusion.14 = (bf16[768,128]{1,0:T(8,128)(2,1)S(1)}, f32[768,128]{1,0:T(8,128)S(1)}) fusion(bf16[4096,128]{1,0:T(8,128)(2,1)S(1)} %bitcast.25, bf16[768,1024]{1,0:T(8,128)(2,1)S(1)} %copy-done, bf16[1024,4096]{1,0:T(8,128)(2,1)} %all-gather.2.cloned.1.call-done), kind=kOutput, calls=%fused_computation.25 | convolution fusion | flops 7254147072 | bytes 11599872 | tf_op jit(solution)/shard_map/dot_general | solution.py:66
  205.5 0.0 copy-start.3
  205.6 1.4 broadcast_in_dim.6
  206.9 0.0 copy-start.2
  206.9 11.8 %all-to-all-start.3 = ((bf16[8,768,128]{2,1,0:T(8,128)(2,1)}), bf16[8,768,128]{2,1,0:T(8,128)(2,1)S(1)}, u32[]{:S(2)}, u32[]{:S(2)}) async-start(bf16[8,768,128]{2,1,0:T(8,128)(2,1)} %broadcast_in_dim.6), calls=%async_computation.3 | async-start | bytes 3145728 | tf_op jit(solution)/shard_map/all_to_all | solution.py:38
  218.7 0.0 copy-done.3
  218.7 0.6 fusion.10
  219.3 0.6 dynamic_slice.4
  220.5 0.5 convolution_reduce_fusion.1
  221.0 34.4 %all-to-all-done.3 = bf16[8,768,128]{2,1,0:T(8,128)(2,1)S(1)} async-done(((bf16[8,768,128]{2,1,0:T(8,128)(2,1)}), bf16[8,768,128]{2,1,0:T(8,128)(2,1)S(1)}, u32[]{:S(2)}, u32[]{:S(2)}) %all-to-all-start.3) | async-done | bytes 1572896 | tf_op jit(solution)/shard_map/all_to_all | solution.py:38
  255.4 0.2 convert_reduce_fusion
  255.7 0.0 copy-start.1
  255.7 0.5 convolution_reduce_fusion
  256.1 0.0 copy-done.2
  256.1 1.3 fusion.11
  257.5 1.4 pad_maximum_fusion.1
  258.9 63.6 %all_to_all.39 = f32[64,1,2]{2,1,0:T(1,128)S(1)} all-to-all(f32[64,1,2]{2,1,0:T(1,128)S(1)} %broadcast_in_dim.7), channel_id=1, replica_groups=mesh['dp'=64,'ens'=8] {'dp'}, dimensions={0} | all-to-all | bytes 1024 | tf_op jit(solution)/shard_map/all_to_all | solution.py:38
  322.5 0.1 reduce_sum.49
  322.6 0.6 fusion.13
  324.5 0.0 copy-done.1
  (2 shorter events, 0.1 us)
Async XLA Ops:
  7.2 186.6 %copy-start = (bf16[768,1024]{1,0:T(8,128)(2,1)S(1)}, bf16[768,1024]{1,0:T(8,128)(2,1)}, u32[]{:S(2)}) copy-start(bf16[768,1024]{1,0:T(8,128)(2,1)} %param.5) | copy-start | bytes 4718596
  7.2 186.6 %all-gather.2.cloned.1.call-start = ((), (), s32[]{:S(2)}) async-start(), calls=%async_computation.5 | async-start | bytes 8519680 | tf_op jit(solution)/shard_map/all_gather | solution.py:62
  205.5 13.1 %copy-start.3 = (s32[8]{0:T(128)S(1)}, s32[8]{0:T(128)}, u32[]{:S(2)}) copy-start(s32[8]{0:T(128)} %param.9) | copy-start | bytes 100
  206.9 49.2 %copy-start.2 = (s32[768]{0:T(1024)S(1)}, s32[768]{0:T(1024)}, u32[]{:S(2)}) copy-start(s32[768]{0:T(1024)} %param.6) | copy-start | bytes 9220
  206.9 48.5 %all-to-all-start.3 = ((bf16[8,768,128]{2,1,0:T(8,128)(2,1)}), bf16[8,768,128]{2,1,0:T(8,128)(2,1)S(1)}, u32[]{:S(2)}, u32[]{:S(2)}) async-start(bf16[8,768,128]{2,1,0:T(8,128)(2,1)} %broadcast_in_dim.6), calls=%async_computation.3 | async-start | bytes 3145728 | tf_op jit(solution)/shard_map/all_to_all | solution.py:38
  255.7 68.9 %copy-start.1 = (f32[768,128]{1,0:T(8,128)}, f32[768,128]{1,0:T(8,128)S(1)}, u32[]{:S(2)}) copy-start(f32[768,128]{1,0:T(8,128)S(1)} %broadcast_multiply_fusion) | copy-start | bytes 1179652
Sparse Core Ops, SparseCore 0:
  40.7 153.0 all-gather.1
where the time goes:
time: 334 us
  blocking collectives  144 us (43%)
  waiting for transfers between devices  139 us (42%)
  between operations  18.3 us (5%)
  matrix products  12.7 us (4%)
  starting transfers between devices  11.8 us (4%)
  local copies, waits for them, and re-layouts  4.51 us (1%)
  other arithmetic  3.76 us (1%)
    all_gather x1, waiting for transfers between devices, on_device(): full_first = lax.all_gather(own_first[0], 'dp', axis=0, tiled=True)  104 us
    all_to_all x1, blocking collectives, from_everyone(): return lax.all_to_all(copies, axis, split_axis=0, concat_axis=0, tiled=True)  63.6 us
    all_to_all x2, blocking collectives, several_exchanges(): lax.all_to_all(section, axis, split_axis=0, concat_axis=0, tiled=True)  47.4 us
    all_to_all x1, waiting for transfers between devices, from_everyone(): return lax.all_to_all(copies, axis, split_axis=0, concat_axis=0, tiled=True)  34.4 us
    all_to_all x1, blocking collectives, on_device(): lax.all_to_all(first_weight, 'ens', split_axis=0, concat_axis=2, tiled=True)  32.7 us
    dot_general x1, matrix products, on_device(): jnp.dot(hidden, own_second[0], preferred_element_type=jnp.float32)  11.8 us
    all_to_all x1, starting transfers between devices, from_everyone(): return lax.all_to_all(copies, axis, split_axis=0, concat_axis=0, tiled=True)  11.8 us
  transfers between devices with their start and end apart: 2, of which 2 were waited for; matrix products, arithmetic and copies ran while one was open for 1% of the time, Pallas kernels for 0%

commit v1 on v0

v1 whole, which is shorter than its diff:
```python
import jax
import jax.numpy as jnp
from jax import lax
from jax.experimental import pallas as pl
from jax.experimental.pallas import tpu as pltpu
from jax.sharding import PartitionSpec as P

MESH = pl.DeviceIdType.MESH
NZ, NX, NC, NY, NH = 8, 4, 2, 4, 2
M, R, F = 8, 16, 512
DOCS, D, G = 768, 1024, 128
BLK = DOCS // NY
FH = F // 2
EARLY = 7
KD = NX * NC * R
FWD_LAG, DOT_LAG = 3, 4
LAST = NZ - 1 + DOT_LAG


def kernel(
    thr, valid, emb, w1, w2, mean_out, kept_out, agree_out,
    W, hid, embv, w2v, w2e, acc, msend, mrecv, zsend, zrecv, scs, scr, szs, szr, st, p1, p2s, p2,
    loc, zr_r, zr_s, zl_r, zl_s, zxr_r, zxr_s, zxl_r, zxl_s,
    xl_r, xr_r, xfl_r, xfr_r, x_s, xxl_r, xxr_r, xxfl_r, xxfr_r, d_r, d_s,
    ylv, zlv, sc_r, sc_s, mr_r, mr_s, szr_r, szr_s, zm_r, zm_s, ag_r, ag_s, p1_r, p1_s, p2_r, p2_s,
):
    dp, ens = lax.axis_index("dp"), lax.axis_index("ens")
    z, x, c = dp // (NX * NC), (dp // NC) % NX, dp % NC
    y, zh = ens // NH, ens % NH

    def dev(z=z, x=x, c=c, y=y, zh=zh):
        return ((z * NX + x) * NC + c, y * NH + zh)

    right, left = (x + 1) % NX, (x + NX - 1) % NX
    ring = zh * NZ + z
    up, down = (ring + 1) % (NZ * NH), (ring + NZ * NH - 1) % (NZ * NH)
    up_dev, down_dev = dev(z=up % NZ, zh=up // NZ), dev(z=down % NZ, zh=down // NZ)
    x_right, x_left = dev(x=right), dev(x=left)
    z_right, z_left = dev(z=(z + 1) % NZ), dev(z=(z + NZ - 1) % NZ)
    partner = dev(c=1 - c)
    across = dev(zh=1 - zh)
    y_up, y_down = dev(y=(y + 1) % NY), dev(y=(y + NY - 1) % NY)
    has_right, has_left = z < NZ - 1, z > 0

    def main(zp, xp, g):
        return W.at[pl.ds(0, EARLY), zp, xp, c, :, pl.ds(g * FH, FH)]

    def late(zp, xp, g):
        return W.at[pl.ds(EARLY, M - EARLY), zp, xp, c, :, pl.ds(g * FH, FH)]

    def late_rows(zp):
        return W.at[pl.ds(EARLY, M - EARLY), zp, :, c]

    def put(ref, send, recv, to, dst=None):
        return pltpu.make_async_remote_copy(
            src_ref=ref, dst_ref=ref if dst is None else dst, send_sem=send, recv_sem=recv,
            device_id=to, device_id_type=MESH)

    def landed(ref, recv):
        put(ref, x_s.at[0], recv, partner).wait_recv()

    def sent(ref, send):
        put(ref, send, d_r.at[0], partner).wait_send()

    barrier = pltpu.get_barrier_semaphore()
    for to in (partner, x_right, x_left, y_up, y_down, up_dev, down_dev):
        pl.semaphore_signal(barrier, inc=1, device_id=to, device_id_type=MESH)
    own_w1 = pltpu.make_async_copy(w1, W.at[:, z, x, c], loc.at[0])
    own_w1.start()
    embs = [pltpu.make_async_copy(emb.at[:, pl.ds(k * KD, KD)], embv.at[k], loc.at[2 + k]) for k in range(NZ)]
    own_w2 = pltpu.make_async_copy(w2, w2v, loc.at[1])
    own_w1.wait()
    pl.semaphore_wait(barrier, 7)

    def send_x(piece, zp, rows, lrecv, rrecv):
        for g in (0, 1):
            put(piece(zp, x, g), x_s.at[0], lrecv.at[rows, g], x_right).start()
            put(piece(zp, x, 1 - g), x_s.at[1], rrecv.at[rows, 1 - g], x_left).start()

    def send_d(ref, zp):
        put(ref, d_s.at[zp], d_r.at[zp], partner).start()

    send_x(late, z, 0, xxl_r, xxr_r)
    for g in (0, 1):
        @pl.when(has_right)
        def _():
            put(main(z, x, g), zr_s.at[0, g], zr_r.at[0, g], z_right).start()

        @pl.when(has_left)
        def _():
            put(main(z, x, g), zl_s.at[0, g], zl_r.at[0, g], z_left).start()
    send_x(main, z, z, xl_r, xr_r)
    for g in (0, 1):
        send_d(main(z, x, g), z)
    pl.semaphore_signal(ylv.at[0], inc=1, device_id=y_up, device_id_type=MESH)
    pl.semaphore_signal(ylv.at[1], inc=1, device_id=y_down, device_id_type=MESH)
    for e in embs:
        e.start()
    own_w2.start()

    def clear(k, carry):
        hid[k // 3, pl.ds((k % 3) * 256, 256), :] = jnp.zeros((256, F), jnp.float32)
        return carry

    lax.fori_loop(0, 3 * M, clear, 0)
    own_w2.wait()

    lane = lax.broadcasted_iota(jnp.int32, (F, G), 1)
    grades = (2.0 * lane.astype(jnp.float32) / (G - 1) - 1.0) * jnp.sqrt(jnp.float32(3.0 / G))

    def extend(e, carry):
        rows = w2v[e]
        col = jnp.sum(rows.astype(jnp.float32) * grades, axis=1, keepdims=True)
        hi = col.astype(jnp.bfloat16).astype(jnp.float32)
        mid = (col - hi).astype(jnp.bfloat16).astype(jnp.float32)
        low = col - hi - mid
        part = jnp.where(lane == e, hi, 0.0) + jnp.where(lane == e + M, mid, 0.0) + jnp.where(lane == e + 2 * M, low, 0.0)
        w2e[e, :, :G] = rows
        w2e[e, :, G:] = part.astype(jnp.bfloat16)
        return carry

    lax.fori_loop(0, M, extend, 0)
    for e in embs:
        e.wait()
    pl.semaphore_wait(ylv.at[0], 1)
    pl.semaphore_wait(ylv.at[1], 1)

    near = jnp.minimum(z, NZ - 1 - z)

    def order(i):
        s = (i + 1) // 2
        both = jnp.where(i % 2 == 1, z - s, z + s)
        return jnp.where(i <= 2 * near, both, jnp.where(z < NZ // 2, i, NZ - 1 - i))

    def z_stage(t, zp, there, on, onward, recv, send):
        @pl.when((t < NZ) & there)
        def _():
            for g in (0, 1):
                landed(main(zp, x, g), recv.at[t - 1, g])

                @pl.when(on)
                def _():
                    put(main(zp, x, g), send.at[t, g], recv.at[t, g], onward).start()
            send_x(main, zp, zp, xl_r, xr_r)
            for g in (0, 1):
                send_d(main(zp, x, g), zp)

    def late_stage(s, zp, there, on, onward, recv, send):
        @pl.when((s >= 1) & (s < NZ) & there)
        def _():
            landed(late_rows(zp), recv.at[s - 1])

            @pl.when(on)
            def _():
                put(late_rows(zp), send.at[s], recv.at[s], onward).start()
            send_d(late_rows(zp), zp)

    def step(t, carry):
        @pl.when(t < NZ)
        def _():
            pl.semaphore_signal(zlv.at[0], inc=1, device_id=up_dev, device_id_type=MESH)
            pl.semaphore_signal(zlv.at[1], inc=1, device_id=down_dev, device_id_type=MESH)
        z_stage(t, z - t, z - t >= 0, has_right, z_right, zr_r, zr_s)
        z_stage(t, z + t, z + t < NZ, has_left, z_left, zl_r, zl_s)

        @pl.when(t == 1)
        def _():
            landed(late(z, left, 0), xxl_r.at[0, 0])
            put(late(z, left, 0), x_s.at[2], xxfl_r.at[0], x_right).start()
            landed(late(z, right, 1), xxr_r.at[0, 1])
            put(late(z, right, 1), x_s.at[3], xxfr_r.at[0], x_left).start()
            landed(late(z, left, 1), xxl_r.at[0, 1])
            landed(late(z, right, 0), xxr_r.at[0, 0])
            landed(late(z, (x + 2) % NX, 0), xxfl_r.at[0])
            landed(late(z, (x + 2) % NX, 1), xxfr_r.at[0])

            @pl.when(has_right)
            def _():
                put(late_rows(z), zxr_s.at[0], zxr_r.at[0], z_right).start()

            @pl.when(has_left)
            def _():
                put(late_rows(z), zxl_s.at[0], zxl_r.at[0], z_left).start()
            send_d(late_rows(z), z)

        late_stage(t - 1, z - t + 1, z - t + 1 >= 0, has_right, z_right, zxr_r, zxr_s)
        late_stage(t - 1, z + t - 1, z + t - 1 < NZ, has_left, z_left, zxl_r, zxl_s)

        @pl.when(t <= NZ)
        def _():
            zp = order(t - 1)
            landed(main(zp, left, 0), xl_r.at[zp, 0])
            put(main(zp, left, 0), x_s.at[2], xfl_r.at[zp], x_right).start()
            landed(main(zp, right, 1), xr_r.at[zp, 1])
            put(main(zp, right, 1), x_s.at[3], xfr_r.at[zp], x_left).start()
            landed(main(zp, left, 1), xl_r.at[zp, 1])
            landed(main(zp, right, 0), xr_r.at[zp, 0])
            for g in (0, 1):
                send_d(main(zp, left, g), zp)
                send_d(main(zp, right, g), zp)

        @pl.when((t >= FWD_LAG) & (t < NZ + FWD_LAG))
        def _():
            zp = order(t - FWD_LAG)
            landed(main(zp, (x + 2) % NX, 0), xfl_r.at[zp])
            landed(main(zp, (x + 2) % NX, 1), xfr_r.at[zp])
            for g in (0, 1):
                send_d(main(zp, (x + 2) % NX, g), zp)

        @pl.when((t >= DOT_LAG) & (t < NZ + DOT_LAG))
        def _():
            zp = order(t - DOT_LAG)
            landed(W.at[:, zp, :, 1 - c], d_r.at[zp])

            def one(k, carry):
                e, rows = k // 3, pl.ds((k % 3) * 256, 256)
                block = W[e, zp].reshape(KD, F)
                hid[e, rows, :] += jnp.dot(embv[zp, rows, :], block, preferred_element_type=jnp.float32)
                return carry

            lax.fori_loop(0, 3 * M, one, 0)

        @pl.when(t < NZ)
        def _():
            pl.semaphore_wait(zlv.at[0], 1)
            pl.semaphore_wait(zlv.at[1], 1)
        return carry

    lax.fori_loop(1, LAST + 1, step, 0)

    acc[pl.ds(DOCS, 64), :] = jnp.zeros((64, 2 * G), jnp.float32)

    def second(k, carry):
        rows = pl.ds(k * 128, 128)
        total = None
        for e in range(M):
            h = jnp.maximum(hid[e, rows, :], 0.0).astype(jnp.bfloat16)
            p = jnp.dot(h, w2e[e], preferred_element_type=jnp.float32)
            total = p if total is None else total + p
        acc[rows, :] = total
        msend[rows, :] = total[:, :G].astype(jnp.bfloat16)
        return carry

    lax.fori_loop(0, DOCS // 128, second, 0)

    for k in range(NY):
        cols = acc[pl.ds(k * BLK, 256), G:].T
        scs[k] = cols[0:M] + cols[M:2 * M] + cols[2 * M:3 * M]

    def y_peer(k):
        return (y + k) % NY

    def y_rows(k):
        return pl.ds(pl.multiple_of(k * BLK, BLK), BLK)

    for k in range(1, NY):
        put(scs.at[y_peer(k)], sc_s, sc_r, dev(y=y_peer(k)), scr.at[y]).start()
    for k in range(1, NY):
        put(msend.at[y_rows(y_peer(k))], mr_s, mr_r, dev(y=y_peer(k)), mrecv.at[y]).start()

    landed(scr.at[pl.ds(0, NY - 1)], sc_r)
    szs[...] = scs[y] + (scr[y_peer(1)] + scr[y_peer(2)] + scr[y_peer(3)])
    put(szs, szr_s, szr_r, across, szr).start()

    landed(mrecv.at[pl.ds(0, NY - 1)], mr_r)
    part = acc[y_rows(y), :G]
    for k in range(1, NY):
        part = part + mrecv[y_peer(k)].astype(jnp.float32)
    zsend[...] = part.astype(jnp.bfloat16)
    put(zsend, zm_s, zm_r, across, zrecv).start()

    member = lax.broadcasted_iota(jnp.int32, (M, 1), 0)
    cut, mean_cut = jnp.zeros((M, 1), jnp.float32), 0.0
    for e in range(M):
        te = thr[e].astype(jnp.float32) / 256.0
        cut = jnp.where(member == e, te, cut)
        mean_cut = mean_cut + te
    mean_cut = mean_cut / M
    landed(szr, szr_r)
    scores = szs[...] + szr[...]
    kept = valid[pl.ds(y, 1), :] * jax.nn.sigmoid(4.0 * (scores - cut))
    ens_score = jnp.sum(scores, axis=0, keepdims=True) / M
    agree = kept * jax.nn.sigmoid(4.0 * (ens_score - mean_cut))
    kept_sum = jnp.sum(kept, axis=1, keepdims=True)
    agree_sum = jnp.sum(agree, axis=1, keepdims=True)
    lane8 = lax.broadcasted_iota(jnp.int32, (M, G), 1)
    table = jnp.where(lane8 == 0, kept_sum, jnp.where(lane8 == 1, agree_sum, 0.0))
    for e in range(M):
        st[e] = table[e:e + 1]
    mine = (y * NX + x) * NC + c
    p1[mine] = st[ens]

    def share(k, carry):
        q = (mine + k) % (NY * NX * NC)
        yp, xp, cp = q // (NX * NC), (q // NC) % NX, q % NC
        put(st.at[yp * NH + zh], p1_s, p1_r, dev(y=yp, x=xp, c=cp), p1.at[mine]).start()
        return carry

    lax.fori_loop(1, NY * NX * NC, share, 0)

    landed(zrecv, zm_r)
    mean_out[y_rows(y), :] = (zsend[...].astype(jnp.float32) + zrecv[...].astype(jnp.float32)) * (1.0 / M)
    for k in range(1, NY):
        put(mean_out.at[y_rows(y)], ag_s, ag_r, dev(y=y_peer(k))).start()

    landed(p1.at[pl.ds(0, NY * NX * NC - 1)], p1_r)
    p2s[...] = jnp.sum(p1[...], axis=0)
    p2[z] = p2s[...]
    for k in range(1, NZ):
        put(p2s, p2_s, p2_r, dev(z=(z + k) % NZ), p2.at[z]).start()

    landed(mean_out.at[pl.ds(0, DOCS - BLK)], ag_r)
    landed(p2.at[pl.ds(0, NZ - 1)], p2_r)
    total = jnp.sum(p2[...], axis=0) * (1.0 / DOCS)
    kept_out[0] = total[0, 0]
    agree_out[0] = total[0, 1]

    for s in range(NZ - 1):
        @pl.when(has_right & (s <= z))
        def _():
            for g in (0, 1):
                sent(main(0, 0, g), zr_s.at[s, g])
            sent(late_rows(0), zxr_s.at[s])

        @pl.when(has_left & (z + s < NZ))
        def _():
            for g in (0, 1):
                sent(main(0, 0, g), zl_s.at[s, g])
            sent(late_rows(0), zxl_s.at[s])
    for k in (0, 1):
        sent(W.at[pl.ds(0, EARLY), :, 0, 0], x_s.at[k])
        sent(W.at[pl.ds(EARLY, M - EARLY), 0, 0, 0], x_s.at[k])
        sent(W.at[pl.ds(0, EARLY), :, 0, 0, :, pl.ds(0, FH)], x_s.at[2 + k])
        sent(W.at[pl.ds(EARLY, M - EARLY), 0, 0, 0, :, pl.ds(0, FH)], x_s.at[2 + k])
    for k in range(NZ):
        sent(W.at[:, k, :, 0], d_s.at[k])
    sent(scr.at[pl.ds(0, NY - 1)], sc_s)
    sent(mrecv.at[pl.ds(0, NY - 1)], mr_s)
    sent(szs, szr_s)
    sent(zsend, zm_s)
    sent(mean_out.at[pl.ds(0, DOCS - BLK)], ag_s)
    sent(p1.at[pl.ds(0, NY * NX * NC - 1)], p1_s)
    sent(p2.at[pl.ds(0, NZ - 1)], p2_s)


def on_device(embeddings, valid_mask, first_weight, second_weight, thresholds):
    valid = jnp.pad(valid_mask.reshape(NY, BLK).astype(jnp.float32), ((0, 0), (0, 256 - BLK)))
    dma, reg = pltpu.SemaphoreType.DMA, pltpu.SemaphoreType.REGULAR
    f32, bf16 = jnp.float32, jnp.bfloat16
    vmem = pl.BlockSpec(memory_space=pltpu.VMEM)
    smem = pl.BlockSpec(memory_space=pltpu.SMEM)
    hbm = pl.BlockSpec(memory_space=pl.ANY)
    mean, kept, agree = pl.pallas_call(
        kernel,
        out_shape=(
            jax.ShapeDtypeStruct((DOCS, G), f32),
            jax.ShapeDtypeStruct((1,), f32),
            jax.ShapeDtypeStruct((1,), f32),
        ),
        in_specs=[smem, vmem, hbm, hbm, hbm],
        out_specs=(vmem, smem, smem),
        scratch_shapes=[
            pltpu.VMEM((M, NZ, NX, NC, R, F), bf16),
            pltpu.VMEM((M, DOCS, F), f32),
            pltpu.VMEM((NZ, DOCS, KD), bf16),
            pltpu.VMEM((M, F, G), bf16),
            pltpu.VMEM((M, F, 2 * G), bf16),
            pltpu.VMEM((DOCS + 64, 2 * G), f32),
            pltpu.VMEM((DOCS, G), bf16),
            pltpu.VMEM((NY, BLK, G), bf16),
            pltpu.VMEM((BLK, G), bf16),
            pltpu.VMEM((BLK, G), bf16),
            pltpu.VMEM((NY, M, 256), f32),
            pltpu.VMEM((NY, M, 256), f32),
            pltpu.VMEM((M, 256), f32),
            pltpu.VMEM((M, 256), f32),
            pltpu.VMEM((M, 1, G), f32),
            pltpu.VMEM((NY * NX * NC, 1, G), f32),
            pltpu.VMEM((1, G), f32),
            pltpu.VMEM((NZ, 1, G), f32),
            dma((2 + NZ,)),
            dma((NZ, 2)), dma((NZ, 2)), dma((NZ, 2)), dma((NZ, 2)),
            dma((NZ,)), dma((NZ,)), dma((NZ,)), dma((NZ,)),
            dma((NZ, 2)), dma((NZ, 2)), dma((NZ,)), dma((NZ,)), dma((4,)),
            dma((1, 2)), dma((1, 2)), dma((1,)), dma((1,)), dma((NZ,)), dma((NZ,)),
            reg((2,)), reg((2,)),
            dma, dma, dma, dma, dma, dma, dma, dma, dma, dma, dma, dma, dma, dma,
        ],
        compiler_params=pltpu.CompilerParams(
            collective_id=0, has_side_effects=True, vmem_limit_bytes=56 * 1024 * 1024
        ),
    )(thresholds, valid, embeddings, first_weight, second_weight)
    return mean, kept, agree


def solution(mesh):
    return jax.shard_map(
        on_device,
        mesh=mesh,
        in_specs=(P("dp", None), P("dp"), P(None, "dp", "ens"), P(None, "ens", None), P()),
        out_specs=(P("dp", None), P("ens"), P("ens")),
        check_vma=False,
    )
```

time: 334 us -> 114 us (0.34)
  blocking collectives: 144 us -> 0 us
  waiting for transfers between devices: 139 us -> 0 us
  Pallas kernels: 0 us -> 106 us
  between operations: 18.3 us -> 4.21 us
  matrix products: 12.7 us -> 0 us
  starting transfers between devices: 11.8 us -> 0 us
    all_to_all x4 -> x0, blocking collectives: 144 us -> none  [the longest x1 63.6 us: from_everyone(): return lax.all_to_all(copies, axis, split_axis=0, concat_axis=0, tiled=True)]
    pallas_call x0 -> x1, Pallas kernels: none -> 106 us  [on_device(): pl.pallas_call(kernel, out_shape=(jax.ShapeDtypeStruct((DOCS, G), f32), j...]
    all_gather x1 -> x0, waiting for transfers between devices: 104 us -> none  [on_device(): full_first = lax.all_gather(own_first[0], 'dp', axis=0, tiled=True)]
    all_to_all x1 -> x0, waiting for transfers between devices: 34.4 us -> none  [from_everyone(): return lax.all_to_all(copies, axis, split_axis=0, concat_axis=0, tiled=True)]
    dot_general x3 -> x0, matrix products: 12.7 us -> none  [the longest x1 11.8 us: on_device(): jnp.dot(hidden, own_second[0], preferred_element_type=jnp.float32)]
    all_to_all x1 -> x0, starting transfers between devices: 11.8 us -> none  [from_everyone(): return lax.all_to_all(copies, axis, split_axis=0, concat_axis=0, tiled=True)]
  transfers between devices with their start and end apart: 2 -> 0, of which waited for: 2 -> 0; matrix products, arithmetic and copies ran while one was open for 1% -> 0% of each run, Pallas kernels for 0% -> 0%
where the time goes in v1:
time: 114 us; the launch traced here: 113 us
  Pallas kernels  106 us (93%)
  between operations  4.21 us (4%)
  local copies, waits for them, and re-layouts  2.45 us (2%)
    pallas_call x1, Pallas kernels, on_device(): pl.pallas_call(kernel, out_shape=(jax.ShapeDtypeStruct((DOCS, G), f32), j...  106 us

profile of v1, /device:TPU:1, one launch (start us, length us, event | category | flops | bytes accessed | tf_op | source)
XLA Modules:
  0.0 113.4 jit_solution(1054386425700019482)
XLA Ops:
  0.6 0.7 convert_element_type.8
  1.3 0.1 convert_element_type.9
  1.4 0.6 pad.4.valid
  2.0 106.0 %shard_map.76 = (f32[768,128]{1,0:T(8,128)}, f32[1]{0:T(128)}, f32[1]{0:T(128)}) custom-call(s32[8]{0:T(128)} %thr.1, f32[4,256]{1,0:T(4,128)} %pad.4.valid, bf16[768,1024]{1,0:T(8,128)(2,1)} %emb.1, bf16[8,16,512]{2,1,0:T(8,128)(2,1)} %w1.1, bf16[8,512,128]{2,1,0:T(8,128)(2,1)} %w2.1), custom_call_target="tpu_custom_call" | custom-call | tf_op jit(solution)/shard_map/pallas_call | solution.py:353
  108.0 1.8 %copy.11 = f32[768,128]{1,0:T(8,128)} copy(f32[768,128]{1,0:T(8,128)} %get-tuple-element.6) | data formatting | bytes 786432

commit v2 on v1

v2 whole, which is shorter than its diff:
```python
import jax
import jax.numpy as jnp
from jax import lax
from jax.experimental import pallas as pl
from jax.experimental.pallas import tpu as pltpu
from jax.sharding import PartitionSpec as P

MESH = pl.DeviceIdType.MESH
NZ, NX, NC, NY, NH = 8, 4, 2, 4, 2
M, R, F = 8, 16, 512
DOCS, D, G = 768, 1024, 128
BLK = DOCS // NY
FH = F // 2
EARLY = 7
KD = NX * NC * R
FWD_LAG, DOT_LAG = 3, 5
LAST = DOT_LAG + NZ - 3


def kernel(
    thr_in, valid_in, emb, w1, w2, mean_out, kept_out, agree_out,
    thr, valid, W, hid, embv, w2v, w2e, acc, window, msend, mrecv, zsend, zrecv, whole, scs, scr, szs, szr, st, p1, p2s, p2,
    loc, zr_r, zr_s, zl_r, zl_s, zxr_r, zxr_s, zxl_r, zxl_s,
    xl_r, xr_r, xfl_r, xfr_r, x_s, xxl_r, xxr_r, xxfl_r, xxfr_r, d_r, d_s,
    ylv, zlv, sc_r, sc_s, mr_r, mr_s, szr_r, szr_s, zm_r, zm_s, ag_r, ag_s, p1_r, p1_s, p2_r, p2_s,
):
    dp, ens = lax.axis_index("dp"), lax.axis_index("ens")
    z, x, c = dp // (NX * NC), (dp // NC) % NX, dp % NC
    y, zh = ens // NH, ens % NH

    def dev(z=z, x=x, c=c, y=y, zh=zh):
        return ((z * NX + x) * NC + c, y * NH + zh)

    right, left = (x + 1) % NX, (x + NX - 1) % NX
    ring = zh * NZ + z
    up, down = (ring + 1) % (NZ * NH), (ring + NZ * NH - 1) % (NZ * NH)
    up_dev, down_dev = dev(z=up % NZ, zh=up // NZ), dev(z=down % NZ, zh=down // NZ)
    x_right, x_left = dev(x=right), dev(x=left)
    z_right, z_left = dev(z=(z + 1) % NZ), dev(z=(z + NZ - 1) % NZ)
    partner = dev(c=1 - c)
    across = dev(zh=1 - zh)
    y_up, y_down = dev(y=(y + 1) % NY), dev(y=(y + NY - 1) % NY)
    has_right, has_left = z < NZ - 1, z > 0

    def main(zp, xp, g):
        return W.at[pl.ds(0, EARLY), zp, xp, c, :, pl.ds(g * FH, FH)]

    def shard(zp, xp):
        return W.at[pl.ds(0, EARLY), zp, xp, c]

    def late(zp, xp, g):
        return W.at[pl.ds(EARLY, M - EARLY), zp, xp, c, :, pl.ds(g * FH, FH)]

    def late_rows(zp):
        return W.at[pl.ds(EARLY, M - EARLY), zp, :, c]

    def put(ref, send, recv, to, dst=None):
        return pltpu.make_async_remote_copy(
            src_ref=ref, dst_ref=ref if dst is None else dst, send_sem=send, recv_sem=recv,
            device_id=to, device_id_type=MESH)

    def landed(ref, recv):
        put(ref, x_s.at[0], recv, partner).wait_recv()

    def sent(ref, send):
        put(ref, send, d_r.at[0], partner).wait_send()

    barrier = pltpu.get_barrier_semaphore()
    for to in (partner, x_right, x_left, y_up, y_down, up_dev, down_dev):
        pl.semaphore_signal(barrier, inc=1, device_id=to, device_id_type=MESH)
    own_w1 = pltpu.make_async_copy(w1, W.at[:, z, x, c], loc.at[0])
    own_w1.start()
    embs = [pltpu.make_async_copy(emb.at[:, pl.ds(k * KD, KD)], embv.at[k], loc.at[2 + k]) for k in range(NZ)]
    own_w2 = pltpu.make_async_copy(w2, w2v, loc.at[1])
    small = [pltpu.make_async_copy(thr_in, thr, loc.at[2 + NZ]), pltpu.make_async_copy(valid_in, valid, loc.at[3 + NZ])]
    own_w1.wait()
    pl.semaphore_wait(barrier, 7)

    def send_x(piece, zp, rows, lrecv, rrecv):
        for g in (0, 1):
            put(piece(zp, x, g), x_s.at[0], lrecv.at[rows, g], x_right).start()
            put(piece(zp, x, 1 - g), x_s.at[1], rrecv.at[rows, 1 - g], x_left).start()

    def send_d(ref, zp):
        put(ref, d_s.at[zp], d_r.at[zp], partner).start()

    send_x(late, z, 0, xxl_r, xxr_r)
    for g in (0, 1):
        @pl.when(has_right)
        def _():
            put(main(z, x, g), zr_s.at[0, g], zr_r.at[0, g], z_right).start()

        @pl.when(has_left)
        def _():
            put(main(z, x, g), zl_s.at[0, g], zl_r.at[0, g], z_left).start()
    send_x(main, z, z, xl_r, xr_r)
    send_d(shard(z, x), z)
    pl.semaphore_signal(ylv.at[0], inc=1, device_id=y_up, device_id_type=MESH)
    pl.semaphore_signal(ylv.at[1], inc=1, device_id=y_down, device_id_type=MESH)
    for e in embs:
        e.start()
    own_w2.start()
    for e in small:
        e.start()

    def clear(k, carry):
        hid[k // 3, pl.ds((k % 3) * 256, 256), :] = jnp.zeros((256, F), jnp.float32)
        return carry

    lax.fori_loop(0, 3 * M, clear, 0)
    window[...] = jnp.zeros((2 * G, G), jnp.float32)
    own_w2.wait()

    lane = lax.broadcasted_iota(jnp.int32, (F, G), 1)
    grades = (2.0 * lane.astype(jnp.float32) / (G - 1) - 1.0) * jnp.sqrt(jnp.float32(3.0 / G))

    def extend(e, carry):
        rows = w2v[e]
        col = jnp.sum(rows.astype(jnp.float32) * grades, axis=1, keepdims=True)
        hi = col.astype(jnp.bfloat16).astype(jnp.float32)
        mid = (col - hi).astype(jnp.bfloat16).astype(jnp.float32)
        low = col - hi - mid
        at = (e % NH) * NY + e // NH
        part = jnp.where(lane == at, hi, 0.0) + jnp.where(lane == at + M, mid, 0.0) + jnp.where(lane == at + 2 * M, low, 0.0)
        w2e[e, :, :G] = rows
        w2e[e, :, G:] = part.astype(jnp.bfloat16)
        return carry

    lax.fori_loop(0, M, extend, 0)
    landed(late(z, left, 0), xxl_r.at[0, 0])
    put(late(z, left, 0), x_s.at[2], xxfl_r.at[0], x_right).start()
    landed(late(z, right, 1), xxr_r.at[0, 1])
    put(late(z, right, 1), x_s.at[3], xxfr_r.at[0], x_left).start()
    pl.semaphore_wait(ylv.at[0], 1)
    pl.semaphore_wait(ylv.at[1], 1)

    near = jnp.minimum(z, NZ - 1 - z)

    def order(i):
        s = (i + 1) // 2
        both = jnp.where(i % 2 == 1, z - s, z + s)
        return jnp.where(i <= 2 * near, both, jnp.where(z < NZ // 2, i, NZ - 1 - i))

    def z_stage(t, zp, there, on, onward, recv, send):
        @pl.when((t < NZ) & there)
        def _():
            for g in (0, 1):
                landed(main(zp, x, g), recv.at[t - 1, g])

                @pl.when(on)
                def _():
                    put(main(zp, x, g), send.at[t, g], recv.at[t, g], onward).start()
            send_x(main, zp, zp, xl_r, xr_r)
            send_d(shard(zp, x), zp)

    def late_stage(s, zp, there, on, onward, recv, send):
        @pl.when((s >= 1) & (s < NZ) & there)
        def _():
            landed(late_rows(zp), recv.at[s - 1])

            @pl.when(on)
            def _():
                put(late_rows(zp), send.at[s], recv.at[s], onward).start()
            send_d(late_rows(zp), zp)

    def joined(p):
        for zp in (order(2 * p), order(2 * p + 1)):
            landed(W.at[:, zp, :, 1 - c], d_r.at[zp])

    def dots(p, e):
        za, zb = order(2 * p), order(2 * p + 1)
        block = jnp.concatenate([W[e, za].reshape(KD, F), W[e, zb].reshape(KD, F)], axis=0)

        lhs = jnp.concatenate([embv[za], embv[zb]], axis=1)
        hid[e] += jnp.dot(lhs, block, preferred_element_type=jnp.float32)

    def quarter(t, j):
        @pl.when(t >= DOT_LAG)
        def _():
            p, half = (t - DOT_LAG) // 2, (t - DOT_LAG) % 2
            if j == 0:
                @pl.when(t == DOT_LAG)
                def _():
                    for e in embs + small:
                        e.wait()

                @pl.when(half == 0)
                def _():
                    joined(p)
            dots(p, half * (M // 2) + j)

    def step(t, carry):
        @pl.when(t < NZ)
        def _():
            pl.semaphore_signal(zlv.at[0], inc=1, device_id=up_dev, device_id_type=MESH)
            pl.semaphore_signal(zlv.at[1], inc=1, device_id=down_dev, device_id_type=MESH)
        z_stage(t, z - t, z - t >= 0, has_right, z_right, zr_r, zr_s)
        z_stage(t, z + t, z + t < NZ, has_left, z_left, zl_r, zl_s)

        quarter(t, 0)

        late_stage(t - 1, z - t + 1, z - t + 1 >= 0, has_right, z_right, zxr_r, zxr_s)
        late_stage(t - 1, z + t - 1, z + t - 1 < NZ, has_left, z_left, zxl_r, zxl_s)

        quarter(t, 1)

        @pl.when(t <= NZ)
        def _():
            zp = order(t - 1)
            landed(main(zp, left, 0), xl_r.at[zp, 0])
            put(main(zp, left, 0), x_s.at[2], xfl_r.at[zp], x_right).start()
            landed(main(zp, right, 1), xr_r.at[zp, 1])
            put(main(zp, right, 1), x_s.at[3], xfr_r.at[zp], x_left).start()
            landed(main(zp, left, 1), xl_r.at[zp, 1])
            landed(main(zp, right, 0), xr_r.at[zp, 0])
            send_d(shard(zp, left), zp)
            send_d(shard(zp, right), zp)

        quarter(t, 2)

        @pl.when((t >= FWD_LAG) & (t < NZ + FWD_LAG))
        def _():
            zp = order(t - FWD_LAG)
            landed(main(zp, (x + 2) % NX, 0), xfl_r.at[zp])
            landed(main(zp, (x + 2) % NX, 1), xfr_r.at[zp])
            send_d(shard(zp, (x + 2) % NX), zp)

        @pl.when(t == 1)
        def _():
            landed(late(z, left, 1), xxl_r.at[0, 1])
            landed(late(z, right, 0), xxr_r.at[0, 0])
            landed(late(z, (x + 2) % NX, 0), xxfl_r.at[0])
            landed(late(z, (x + 2) % NX, 1), xxfr_r.at[0])

            @pl.when(has_right)
            def _():
                put(late_rows(z), zxr_s.at[0], zxr_r.at[0], z_right).start()

            @pl.when(has_left)
            def _():
                put(late_rows(z), zxl_s.at[0], zxl_r.at[0], z_left).start()
            send_d(late_rows(z), z)

        @pl.when(t < NZ)
        def _():
            pl.semaphore_wait(zlv.at[0], 1)
            pl.semaphore_wait(zlv.at[1], 1)
        quarter(t, 3)
        return carry

    lax.fori_loop(1, LAST + 1, step, 0)
    joined(NZ // 2 - 1)

    def y_peer(k):
        return (y + k) % NY

    def last(i, carry):
        b = y_peer(jnp.where(i == 0, 2, jnp.where(i == 1, 1, jnp.where(i == 2, 3, 0))))
        rows = pl.ds(pl.multiple_of(b * BLK, BLK), BLK)
        za, zb = order(NZ - 2), order(NZ - 1)
        lhs = jnp.concatenate([embv[za, rows, :], embv[zb, rows, :]], axis=1)
        total = None
        for e in range(M):
            block = jnp.concatenate([W[e, za].reshape(KD, F), W[e, zb].reshape(KD, F)], axis=0)
            pre = hid[e, rows, :] + jnp.dot(lhs, block, preferred_element_type=jnp.float32)
            h = jnp.maximum(pre, 0.0).astype(jnp.bfloat16)
            p = jnp.dot(h, w2e[e], preferred_element_type=jnp.float32)
            total = p if total is None else total + p
        acc[...] = total[:, :G]
        msend[b] = total[:, :G].astype(jnp.bfloat16)
        window[pl.ds(pl.multiple_of((b % 2) * (2 * G - BLK), 2 * G - BLK), BLK), :] = total[:, G:]
        cols = window[...].T
        scs[b] = cols[0:M] + cols[M:2 * M] + cols[2 * M:3 * M]

        @pl.when(i < NY - 1)
        def _():
            put(scs.at[b], sc_s, sc_r, dev(y=b), scr.at[y]).start()
            put(msend.at[b], mr_s, mr_r, dev(y=b), mrecv.at[y]).start()
        return carry

    lax.fori_loop(0, NY, last, 0)

    landed(scr.at[pl.ds(0, NY - 1)], sc_r)
    mine_y = scs[y] + (scr[y_peer(1)] + scr[y_peer(2)] + scr[y_peer(3)])
    row = y * BLK // G
    lane2 = lax.broadcasted_iota(jnp.int32, (1, 2 * G), 1)
    first = (y % 2) * (2 * G - BLK)
    inside = (lane2 >= first) & (lane2 < first + BLK)
    flags = jnp.concatenate([valid[pl.ds(row, 1), :], valid[pl.ds(row + 1, 1), :]], axis=1).astype(jnp.float32)
    flags = jnp.where(inside, flags, 0.0)
    every = jnp.sum(mine_y, axis=0, keepdims=True)
    half_way = (z + NZ // 2) % NZ
    for h in range(NH):
        szs[h] = jnp.concatenate(
            [mine_y[h * NY:(h + 1) * NY], every, flags, jnp.zeros((2, 2 * G), jnp.float32)], axis=0)
        put(szs.at[h], szr_s, szr_r, dev(z=half_way, zh=h), szr.at[zh]).start()

    landed(mrecv.at[pl.ds(0, NY - 1)], mr_r)
    part = acc[...]
    for k in range(1, NY):
        part = part + mrecv[y_peer(k)].astype(jnp.float32)
    zsend[...] = part.astype(jnp.bfloat16)
    put(zsend, zm_s, zm_r, across, zrecv).start()

    member = lax.broadcasted_iota(jnp.int32, (NY, 1), 0)
    cut, mean_cut = jnp.zeros((NY, 1), jnp.float32), 0.0
    for e in range(M):
        te = thr[e].astype(jnp.float32) / 256.0
        cut = jnp.where((member == e // NH) & (zh == e % NH), te, cut)
        mean_cut = mean_cut + te
    mean_cut = mean_cut / M
    landed(szr, szr_r)
    scores = szr[0] + szr[1]
    kept = szr[0, NY + 1:NY + 2] * jax.nn.sigmoid(4.0 * (scores[0:NY] - cut))
    agree = kept * jax.nn.sigmoid(4.0 * (scores[NY:NY + 1] / M - mean_cut))
    kept_sum = jnp.sum(kept, axis=1, keepdims=True)
    agree_sum = jnp.sum(agree, axis=1, keepdims=True)
    lane4 = lax.broadcasted_iota(jnp.int32, (NY, G), 1)
    table = jnp.where(lane4 == 0, kept_sum, jnp.where(lane4 == 1, agree_sum, 0.0))
    for k in range(NY):
        st[k] = table[k:k + 1]
    mine = (y * NX + x) * NC + c
    p1[mine] = st[y]

    def share(k, carry):
        q = (mine + k) % (NY * NX * NC)
        yp, xp, cp = q // (NX * NC), (q // NC) % NX, q % NC
        put(st.at[yp], p1_s, p1_r, dev(y=yp, x=xp, c=cp), p1.at[mine]).start()
        return carry

    lax.fori_loop(1, NY * NX * NC, share, 0)

    landed(zrecv, zm_r)
    whole[y] = ((zsend[...].astype(jnp.float32) + zrecv[...].astype(jnp.float32)) * (1.0 / M)).astype(jnp.bfloat16)
    for k in range(1, NY):
        put(whole.at[y], ag_s, ag_r, dev(y=y_peer(k))).start()

    landed(p1.at[pl.ds(0, NY * NX * NC - 1)], p1_r)
    p2s[...] = jnp.sum(p1[...], axis=0)
    p2[z] = p2s[...]
    for k in range(1, NZ):
        put(p2s, p2_s, p2_r, dev(z=(z + k) % NZ), p2.at[z]).start()

    landed(whole.at[pl.ds(0, NY - 1)], ag_r)
    out = pltpu.make_async_copy(whole, mean_out, loc.at[0])
    out.start()
    landed(p2.at[pl.ds(0, NZ - 1)], p2_r)
    total = jnp.sum(p2[...], axis=0) * (1.0 / DOCS)
    kept_out[0] = total[0, 0]
    agree_out[0] = total[0, 1]

    out.wait()

    for s in range(NZ - 1):
        @pl.when(has_right & (s <= z))
        def _():
            for g in (0, 1):
                sent(main(0, 0, g), zr_s.at[s, g])
            sent(late_rows(0), zxr_s.at[s])

        @pl.when(has_left & (z + s < NZ))
        def _():
            for g in (0, 1):
                sent(main(0, 0, g), zl_s.at[s, g])
            sent(late_rows(0), zxl_s.at[s])
    for k in (0, 1):
        sent(W.at[pl.ds(0, EARLY), :, 0, 0], x_s.at[k])
        sent(W.at[pl.ds(EARLY, M - EARLY), 0, 0, 0], x_s.at[k])
        sent(W.at[pl.ds(0, EARLY), :, 0, 0, :, pl.ds(0, FH)], x_s.at[2 + k])
        sent(W.at[pl.ds(EARLY, M - EARLY), 0, 0, 0, :, pl.ds(0, FH)], x_s.at[2 + k])
    for k in range(NZ):
        sent(W.at[:, k, :, 0], d_s.at[k])
    sent(scr.at[pl.ds(0, NY - 1)], sc_s)
    sent(mrecv.at[pl.ds(0, NY - 1)], mr_s)
    sent(szs, szr_s)
    sent(zsend, zm_s)
    sent(whole.at[pl.ds(0, NY - 1)], ag_s)
    sent(p1.at[pl.ds(0, NY * NX * NC - 1)], p1_s)
    sent(p2.at[pl.ds(0, NZ - 1)], p2_s)


def on_device(embeddings, valid_mask, first_weight, second_weight, thresholds):
    valid = valid_mask.reshape(DOCS // G, G)
    dma, reg = pltpu.SemaphoreType.DMA, pltpu.SemaphoreType.REGULAR
    f32, bf16 = jnp.float32, jnp.bfloat16
    smem = pl.BlockSpec(memory_space=pltpu.SMEM)
    hbm = pl.BlockSpec(memory_space=pltpu.HBM)
    mean, kept, agree = pl.pallas_call(
        kernel,
        out_shape=(
            jax.ShapeDtypeStruct((NY, BLK, G), bf16),
            jax.ShapeDtypeStruct((1,), f32),
            jax.ShapeDtypeStruct((1,), f32),
        ),
        in_specs=[hbm] * 5,
        out_specs=(hbm, smem, smem),
        scratch_shapes=[
            pltpu.SMEM((M,), jnp.int32),
            pltpu.VMEM((DOCS // G, G), jnp.int32),
            pltpu.VMEM((M, NZ, NX, NC, R, F), bf16),
            pltpu.VMEM((M, DOCS, F), f32),
            pltpu.VMEM((NZ, DOCS, KD), bf16),
            pltpu.VMEM((M, F, G), bf16),
            pltpu.VMEM((M, F, 2 * G), bf16),
            pltpu.VMEM((BLK, G), f32),
            pltpu.VMEM((2 * G, G), f32),
            pltpu.VMEM((NY, BLK, G), bf16),
            pltpu.VMEM((NY, BLK, G), bf16),
            pltpu.VMEM((BLK, G), bf16),
            pltpu.VMEM((BLK, G), bf16),
            pltpu.VMEM((NY, BLK, G), bf16),
            pltpu.VMEM((NY, M, 256), f32),
            pltpu.VMEM((NY, M, 256), f32),
            pltpu.VMEM((NH, M, 256), f32),
            pltpu.VMEM((NH, M, 256), f32),
            pltpu.VMEM((NY, 1, G), f32),
            pltpu.VMEM((NY * NX * NC, 1, G), f32),
            pltpu.VMEM((1, G), f32),
            pltpu.VMEM((NZ, 1, G), f32),
            dma((4 + NZ,)),
            dma((NZ, 2)), dma((NZ, 2)), dma((NZ, 2)), dma((NZ, 2)),
            dma((NZ,)), dma((NZ,)), dma((NZ,)), dma((NZ,)),
            dma((NZ, 2)), dma((NZ, 2)), dma((NZ,)), dma((NZ,)), dma((4,)),
            dma((1, 2)), dma((1, 2)), dma((1,)), dma((1,)), dma((NZ,)), dma((NZ,)),
            reg((2,)), reg((2,)),
            dma, dma, dma, dma, dma, dma, dma, dma, dma, dma, dma, dma, dma, dma,
        ],
        compiler_params=pltpu.CompilerParams(
            collective_id=0, has_side_effects=True, vmem_limit_bytes=60 * 1024 * 1024
        ),
    )(thresholds, valid, embeddings, first_weight, second_weight)
    return mean.reshape(DOCS, G).astype(f32), kept, agree


def solution(mesh):
    return jax.shard_map(
        on_device,
        mesh=mesh,
        in_specs=(P("dp", None), P("dp"), P(None, "dp", "ens"), P(None, "ens", None), P()),
        out_specs=(P("dp", None), P("ens"), P("ens")),
        check_vma=False,
    )
```

time: 114 us -> 82.3 us (0.72)
  Pallas kernels: 106 us -> 76.3 us
  local copies, waits for them, and re-layouts: 2.45 us -> 0 us
    pallas_call x1, Pallas kernels: 106 us -> 76.3 us  [on_device(): pl.pallas_call(kernel, out_shape=(jax.ShapeDtypeStruct((NY, BLK, G), bf16...]
    unnamed x1 -> x0, local copies, waits for them, and re-layouts: 1.77 us -> none
where the time goes in v2:
time: 82.3 us; the launch traced here: 82.1 us
  Pallas kernels  76.3 us (93%)
  between operations  4.09 us (5%)
  other arithmetic  1.7 us (2%)
    pallas_call x1, Pallas kernels, on_device(): pl.pallas_call(kernel, out_shape=(jax.ShapeDtypeStruct((NY, BLK, G), bf16...  76.3 us
    convert_element_type x1, other arithmetic, on_device(): return (mean.reshape(DOCS, G).astype(f32), kept, agree)  1.7 us

profile of v2, /device:TPU:1, one launch (start us, length us, event | category | flops | bytes accessed | tf_op | source)
XLA Modules:
  0.0 82.1 jit_solution(3725436925257538906)
XLA Ops:
  0.6 76.3 %shard_map.76 = (bf16[4,192,128]{2,1,0:T(8,128)(2,1)}, f32[1]{0:T(128)}, f32[1]{0:T(128)}) custom-call(s32[8]{0:T(128)} %thr_in.1, s32[6,128]{1,0:T(8,128)} %bitcast.4, bf16[768,1024]{1,0:T(8,128)(2,1)} %emb.1, bf16[8,16,512]{2,1,0:T(8,128)(2,1)} %w1.1, bf16[8,512,128]{2,1,0:T(8,128)(2,1)} %w2.1), custom_call_target="tpu_custom_call" | custom-call | tf_op jit(solution)/shard_map/pallas_call | solution.py:388
  76.9 1.7 %bitcast_convert_fusion = f32[768,128]{1,0:T(8,128)} fusion(bf16[4,192,128]{2,1,0:T(8,128)(2,1)} %get-tuple-element.6), kind=kLoop, calls=%fused_computation | loop fusion | flops 98304 | bytes 589824 | tf_op jit(solution)/shard_map/convert_element_type | solution.py:432
